TPU v7x, 32 devices: a whole 2x2x4 slice. The times are simulated.
32 devices in a mesh: dp: 8 (over z, core), mp: 4 (over y, x).
Axes of the slice: x: 2, y: 2, z: 4, core: 2. Of those that a mesh axis runs over, the one named last changes fastest.
Arguments:
- token_ids: int32 [8192], P('dp'), may hold values from 0 to 128255
- lengths: int32 [64], P('dp'), may hold values from 1 to 128
- embed_grads: bfloat16 [8192, 4096], P('dp', 'mp'), may hold values from -6 to 6
- vocab_basis: bfloat16 [128256, 32], P('mp'), may hold values from -6 to 6
- embed_basis: bfloat16 [4096, 32], P('mp'), may hold values from -0.09375 to 0.09375
- layer_inputs: bfloat16 [1, 8192, 4096], P(None, 'dp', 'mp'), may hold values from -6 to 6
- layer_grads: bfloat16 [1, 8192, 4096], P(None, 'dp', 'mp'), may hold values from -6 to 6
- input_basis: bfloat16 [1, 4096, 32], P(None, 'mp'), may hold values from -0.09375 to 0.09375
- output_basis: bfloat16 [1, 4096, 32], P(None, 'mp'), may hold values from -0.09375 to 0.09375
- queries: bfloat16 [2, 1024, 256], P(None, 'mp', 'dp'), may hold values from -0.19921875 to 0.19921875
Outputs:
- scores: float32 [64, 256], P('dp')
All inputs are finite; a program needn't handle non-finite values.
Results may differ from a plain program's by a relative error of at most 0.0003.
Values may be sent and summed in bfloat16 or wider, within the bound.
No kernel may reach another device: no remote copies, remote signals or barrier semaphores. Data moves between devices by JAX's collectives and lax.ppermute only.
A program may use at most 64 MiB of HBM per device.

v0:
```python
import jax
import jax.numpy as jnp
from jax import lax
from jax.sharding import PartitionSpec as P

ITERS = 2
damping = 0.01
epsilon = 1e-06
highest = lax.Precision.HIGHEST


def solve_columns(right_side, apply_operator, column_norm, column_curve):
    solution = jnp.zeros_like(right_side)
    residual = right_side
    direction = right_side
    norm_now = column_norm(residual)
    for iteration in range(ITERS):
        images = apply_operator(direction)
        step_size = norm_now / (column_curve(direction, images) + epsilon)
        solution = solution + step_size[:, None, :] * direction
        residual = residual - step_size[:, None, :] * images
        norm_next = column_norm(residual)
        direction = residual + (norm_next / (norm_now + epsilon))[:, None, :] * direction
        norm_now = norm_next
    return solution


def per_device(
    token_ids,
    lengths,
    embed_grads,
    vocab_basis,
    embed_basis,
    layer_inputs,
    layer_grads,
    input_basis,
    output_basis,
    queries,
):
    vocab_rows = vocab_basis.shape[0]
    basis_rank = embed_basis.shape[1]
    layer_count = layer_inputs.shape[0] + 1
    seq_count = lengths.shape[0]
    token_count = token_ids.shape[0]
    slot_len = token_count // seq_count
    sketch_len = basis_rank * basis_rank
    mp_index = lax.axis_index("mp")
    local_ids = token_ids - mp_index * vocab_rows
    inside = (local_ids >= 0) & (local_ids < vocab_rows)
    looked = jnp.take(vocab_basis, jnp.clip(local_ids, 0, vocab_rows - 1), axis=0)
    pieces = [
        jnp.dot(embed_grads, embed_basis, preferred_element_type=jnp.float32),
        jnp.where(inside[:, None], looked.astype(jnp.float32), 0.0),
    ]
    pieces.append(jnp.dot(layer_grads[0], output_basis[0], preferred_element_type=jnp.float32))
    pieces.append(jnp.dot(layer_inputs[0], input_basis[0], preferred_element_type=jnp.float32))
    projected = jnp.concatenate(pieces, axis=1)
    inverse_len = 1.0 / lengths.astype(jnp.float32)
    summed = lax.psum(projected, "mp")
    layout = summed.reshape(seq_count, slot_len, layer_count, 2, basis_rank)
    position = jnp.arange(slot_len, dtype=jnp.int32)
    weights = jnp.where(position[None, :] < lengths[:, None], inverse_len[:, None], 0.0)
    weighted = layout[:, :, :, 0, :] * weights[:, :, None, None]
    sketches = jnp.einsum(
        "stli,stlj->lsij", weighted, layout[:, :, :, 1, :], precision=highest
    ).reshape(layer_count, seq_count, sketch_len)
    examples = seq_count * lax.axis_size("dp")
    targets = lax.all_gather(queries, "dp", axis=2, tiled=True)
    everyone = lax.all_gather(sketches, "dp", axis=1, tiled=True)
    columns = lax.all_to_all(targets, "mp", split_axis=2, concat_axis=1, tiled=True)

    def apply_sketch(direction):
        inner_sums = jnp.einsum("lek,lkq->leq", everyone, direction, precision=highest)
        back_proj = jnp.einsum("lek,leq->lkq", everyone, inner_sums, precision=highest)
        return back_proj / examples + damping * direction

    def local_norm(residual):
        return jnp.sum(residual * residual, axis=1)

    def local_curve(direction, images):
        return jnp.sum(direction * images, axis=1)

    solution = solve_columns(columns.astype(jnp.float32), apply_sketch, local_norm, local_curve)
    partial_value = jnp.einsum("lek,lkq->eq", sketches, solution, precision=highest)
    scores = lax.all_gather(partial_value, "mp", axis=1, tiled=True)
    return scores


def solution(mesh):
    placed = (
        P("dp"),
        P("dp"),
        P("dp", "mp"),
        P("mp", None),
        P("mp", None),
        P(None, "dp", "mp"),
        P(None, "dp", "mp"),
        P(None, "mp", None),
        P(None, "mp", None),
        P(None, "mp", "dp"),
    )
    return jax.shard_map(
        per_device, mesh=mesh, in_specs=placed, out_specs=P("dp", None), check_vma=False
    )
```

profile of v0, /device:TPU:0, one launch (start us, length us, event | category | flops | bytes accessed | tf_op | source)
XLA Modules:
  0.0 111.8 jit_solution(4883537781208353662)
XLA Ops:
  6.5 0.0 copy-start
  6.5 0.0 all-reduce.2.cloned.1.call-start
  6.5 0.8 compare_and_fusion.1
  7.4 0.7 fusion.25
  8.1 7.3 %copy.30 = bf16[32064,32]{1,0:T(8,128)(2,1)} copy(bf16[32064,32]{0,1:T(8,128)(2,1)} %param.13) | data formatting | bytes 4104192 | tf_op args[3]
  15.4 0.0 copy-start.3
  15.4 0.0 copy-start.4
  15.4 7.3 %gather_fusion = bf16[1024,32]{1,0:T(8,128)(2,1)S(1)} fusion(bf16[32064,32]{1,0:T(8,128)(2,1)} %copy.30, s32[1024]{0:T(1024)S(1)} %fusion.25), kind=kCustom, calls=%fused_computation | custom fusion | bytes 135168 | tf_op jit(solution)/shard_map/jit(_take)/gather | solution.py:50
  22.7 0.1 copy.31
  22.8 0.0 copy-done
  22.8 0.0 copy-done.3
  22.8 0.0 copy-start.1
  22.8 0.0 copy-start.2
  22.8 0.0 copy-start.5
  22.8 0.7 fusion
  23.6 0.0 copy-done.4
  23.6 0.8 copy-done.1
  24.4 0.7 fusion.2
  25.1 0.0 copy-done.2
  25.1 0.0 copy-done.5
  25.1 0.7 fusion.26
  25.9 0.0 copy-start.6
  25.9 0.0 copy-start.7
  26.0 0.1 copy.38
  26.1 0.9 copy.32
  27.0 0.0 all-reduce.2.cloned.1.call-update
  27.0 0.0 copy-done.6
  27.0 17.0 %all_gather.9 = bf16[2,256,256]{1,0,2:T(2,128)(2,1)} all-gather(bf16[2,256,32]{1,0,2:T(2,128)(2,1)S(1)} %copy.28), channel_id=1, replica_groups=mesh['dp'=8,'mp'=4] {'dp'}, dimensions={2}, use_global_device_ids=true | all-gather | bytes 294912 | tf_op jit(solution)/shard_map/all_gather | solution.py:68
  44.0 3.7 %all-to-all-start = ((bf16[2,256,256]{1,0,2:T(2,128)(2,1)}), bf16[2,256,256]{1,0,2:T(2,128)(2,1)S(1)}, u32[]{:S(2)}, u32[]{:S(2)}) async-start(bf16[2,256,256]{1,0,2:T(2,128)(2,1)} %all_gather.9), calls=%async_computation | async-start | bytes 524288 | tf_op jit(solution)/shard_map/all_to_all | solution.py:70
  47.7 0.0 copy-done.7
  47.8 0.1 fusion.24
  47.8 5.8 %all-to-all-done = bf16[2,256,256]{1,0,2:T(2,128)(2,1)S(1)} async-done(((bf16[2,256,256]{1,0,2:T(2,128)(2,1)}), bf16[2,256,256]{1,0,2:T(2,128)(2,1)S(1)}, u32[]{:S(2)}, u32[]{:S(2)}) %all-to-all-start) | async-done | bytes 262176 | tf_op jit(solution)/shard_map/all_to_all | solution.py:70
  53.6 0.2 copy.42
  53.8 0.2 all_to_all.16
  54.0 0.6 multiply_reduce_fusion.1
  54.6 21.5 %all-reduce.2.cloned.1.call-done = f32[8,128,2,2,32]{1,4,0,2,3:T(8,128)} async-done(((f32[8,128,2,2,32]{1,4,0,2,3:T(8,128)}), f32[8,128,2,2,32]{1,4,0,2,3:T(8,128)}) %all-reduce.2.cloned.1.call-update) | async-done | bytes 524304 | tf_op jit(solution)/shard_map/psum | solution.py:59
  76.0 1.6 %fusion.13 = f32[2,8,32,32]{3,2,1,0:T(8,128)S(1)} fusion(f32[8,128,2,2,32]{1,4,0,2,3:T(8,128)} %all-reduce.2.cloned.1.call-done, f32[8,128]{1,0:T(8,128)S(1)} %fusion.24), kind=kOutput, calls=%fused_computation.25 | convolution fusion | flops 25231360 | bytes 593920 | tf_op jit(solution)/shard_map/stli,stlj->lsij/dot_general | solution.py:64
  77.6 0.1 reshape.68
  77.7 14.7 %all_gather.10 = f32[2,64,1024]{2,1,0:T(8,128)S(1)} all-gather(f32[2,8,1024]{2,1,0:T(8,128)S(1)} %reshape.68), channel_id=1, replica_groups=mesh['dp'=8,'mp'=4] {'dp'}, dimensions={1}, use_global_device_ids=true | all-gather | bytes 589824 | tf_op jit(solution)/shard_map/all_gather | solution.py:69
  92.4 0.4 fusion.27
  92.9 0.8 fusion.8
  93.7 0.2 multiply_reduce_fusion
  93.9 0.7 fusion.19
  94.6 0.8 fusion.7
  95.4 0.7 convolution_bitcast_fusion
  96.1 8.1 %all-gather = f32[4,64,8]{1,2,0:T(8,128)S(1)} all-gather(f32[1,64,8]{1,2,0:T(8,128)S(1)} %convolution_bitcast_fusion), channel_id=1, replica_groups=mesh['dp'=8,'mp'=4] {'mp'}, dimensions={0}, use_global_device_ids=true | all-gather | bytes 10240 | tf_op jit(solution)/shard_map/all_gather | solution.py:85
  104.3 0.7 reshape.79
  (8 shorter events, 0.1 us)
Async XLA Ops:
  6.5 16.2 %copy-start = (bf16[1,1024,1024]{2,1,0:T(8,128)(2,1)S(1)}, bf16[1,1024,1024]{2,1,0:T(8,128)(2,1)}, u32[]{:S(2)}) copy-start(bf16[1,1024,1024]{2,1,0:T(8,128)(2,1)} %param.15) | copy-start | bytes 6291460
  6.5 69.5 %all-reduce.2.cloned.1.call-start = ((), (), s32[]{:S(2)}) async-start(), calls=%async_computation.1 | async-start | bytes 1048576 | tf_op jit(solution)/shard_map/psum | solution.py:59
  15.4 7.4 %copy-start.3 = (bf16[1,1024,32]{1,2,0:T(8,128)(2,1)S(1)}, bf16[1,1024,32]{1,2,0:T(8,128)(2,1)}, u32[]{:S(2)}) copy-start(bf16[1,1024,32]{1,2,0:T(8,128)(2,1)} %param.17) | copy-start | bytes 196612
  15.4 8.2 %copy-start.4 = (bf16[1,1024,32]{1,2,0:T(8,128)(2,1)S(1)}, bf16[1,1024,32]{1,2,0:T(8,128)(2,1)}, u32[]{:S(2)}) copy-start(bf16[1,1024,32]{1,2,0:T(8,128)(2,1)} %param.18) | copy-start | bytes 196612
  22.8 1.6 %copy-start.1 = (bf16[1,1024,1024]{2,1,0:T(8,128)(2,1)S(1)}, bf16[1,1024,1024]{2,1,0:T(8,128)(2,1)}, u32[]{:S(2)}) copy-start(bf16[1,1024,1024]{2,1,0:T(8,128)(2,1)} %param.16) | copy-start | bytes 6291460
  22.8 2.3 %copy-start.2 = (bf16[1024,1024]{1,0:T(8,128)(2,1)S(1)}, bf16[1024,1024]{1,0:T(8,128)(2,1)}, u32[]{:S(2)}) copy-start(bf16[1024,1024]{1,0:T(8,128)(2,1)} %param.12) | copy-start | bytes 6291460
  22.8 2.3 %copy-start.5 = (bf16[1024,32]{0,1:T(8,128)(2,1)S(1)}, bf16[1024,32]{0,1:T(8,128)(2,1)}, u32[]{:S(2)}) copy-start(bf16[1024,32]{0,1:T(8,128)(2,1)} %param.14) | copy-start | bytes 196612
  25.9 1.1 %copy-start.6 = (bf16[2,256,32]{1,2,0:T(8,128)(2,1)S(1)}, bf16[2,256,32]{1,2,0:T(8,128)(2,1)}, u32[]{:S(2)}) copy-start(bf16[2,256,32]{1,2,0:T(8,128)(2,1)} %param.19) | copy-start | bytes 98308
  25.9 21.9 %copy-start.7 = (s32[8]{0:T(128)S(1)}, s32[8]{0:T(128)}, u32[]{:S(2)}) copy-start(s32[8]{0:T(128)} %param.11) | copy-start | bytes 100
  44.0 9.6 %all-to-all-start = ((bf16[2,256,256]{1,0,2:T(2,128)(2,1)}), bf16[2,256,256]{1,0,2:T(2,128)(2,1)S(1)}, u32[]{:S(2)}, u32[]{:S(2)}) async-start(bf16[2,256,256]{1,0,2:T(2,128)(2,1)} %all_gather.9), calls=%async_computation | async-start | bytes 524288 | tf_op jit(solution)/shard_map/all_to_all | solution.py:70
Sparse Core Ops, SparseCore 0:
  27.1 48.8 all-reduce.1
where the time goes:
time: 112 us
  blocking collectives  39.8 us (36%)
  waiting for transfers between devices  27.3 us (24%)
  local copies, waits for them, and re-layouts  17.8 us (16%)
  between operations  13.6 us (12%)
  matrix products  7.11 us (6%)
  starting transfers between devices  3.71 us (3%)
  other arithmetic  2.52 us (2%)
    psum x1, waiting for transfers between devices, per_device(): summed = lax.psum(projected, 'mp')  21.5 us
    all_gather x1, blocking collectives, per_device(): targets = lax.all_gather(queries, 'dp', axis=2, tiled=True)  17 us
    all_gather x1, blocking collectives, per_device(): everyone = lax.all_gather(sketches, 'dp', axis=1, tiled=True)  14.7 us
    unnamed x20, local copies, waits for them, and re-layouts  8.96 us
    all_gather x1, blocking collectives, per_device(): scores = lax.all_gather(partial_value, 'mp', axis=1, tiled=True)  8.14 us
    gather x2, local copies, waits for them, and re-layouts, per_device(): jnp.take(vocab_basis, jnp.clip(local_ids, 0, vocab_rows - 1), axis=0)  7.42 us
    all_to_all x1, waiting for transfers between devices, per_device(): lax.all_to_all(targets, 'mp', split_axis=2, concat_axis=1, tiled=True)  5.79 us
    all_to_all x1, starting transfers between devices, per_device(): lax.all_to_all(targets, 'mp', split_axis=2, concat_axis=1, tiled=True)  3.71 us
  transfers between devices with their start and end apart: 2, of which 2 were waited for; matrix products, arithmetic and copies ran while one was open for 1% of the time, Pallas kernels for 0%

commit v1 on v0

--- a/solution.py
+++ b/solution.py
@@ -56,7 +56,7 @@
     pieces.append(jnp.dot(layer_inputs[0], input_basis[0], preferred_element_type=jnp.float32))
     projected = jnp.concatenate(pieces, axis=1)
     inverse_len = 1.0 / lengths.astype(jnp.float32)
-    summed = lax.psum(projected, "mp")
+    summed = jnp.sum(lax.all_gather(projected, "mp"), axis=0)
     layout = summed.reshape(seq_count, slot_len, layer_count, 2, basis_rank)
     position = jnp.arange(slot_len, dtype=jnp.int32)
     weights = jnp.where(position[None, :] < lengths[:, None], inverse_len[:, None], 0.0)

time: 112 us -> 107 us (0.955)
  waiting for transfers between devices: 27.3 us -> 16.4 us
  other arithmetic: 2.52 us -> 6.2 us
  local copies, waits for them, and re-layouts: 17.8 us -> 20.6 us
    psum x1 -> x0, waiting for transfers between devices: 21.5 us -> none  [per_device(): summed = lax.psum(projected, 'mp')]
    all_gather x0 -> x1, waiting for transfers between devices: none -> 10.6 us  [per_device(): summed = jnp.sum(lax.all_gather(projected, 'mp'), axis=0)]
    all_gather x0 -> x1, local copies, waits for them, and re-layouts: none -> 3.64 us  [per_device(): summed = jnp.sum(lax.all_gather(projected, 'mp'), axis=0)]
    reduce_sum x0 -> x1, other arithmetic: none -> 2.86 us  [per_device(): summed = jnp.sum(lax.all_gather(projected, 'mp'), axis=0)]
where the time goes in v1:
time: 107 us; the launch traced here: 106 us
  blocking collectives  39.8 us (37%)
  local copies, waits for them, and re-layouts  20.6 us (19%)
  waiting for transfers between devices  16.4 us (15%)
  between operations  13.6 us (13%)
  other arithmetic  6.2 us (6%)
  matrix products  6.13 us (6%)
  starting transfers between devices  3.71 us (3%)
    all_gather x1, blocking collectives, per_device(): targets = lax.all_gather(queries, 'dp', axis=2, tiled=True)  17 us
    all_gather x1, blocking collectives, per_device(): everyone = lax.all_gather(sketches, 'dp', axis=1, tiled=True)  14.8 us
    all_gather x1, waiting for transfers between devices, per_device(): summed = jnp.sum(lax.all_gather(projected, 'mp'), axis=0)  10.6 us
    unnamed x20, local copies, waits for them, and re-layouts  8.97 us
    all_gather x1, blocking collectives, per_device(): scores = lax.all_gather(partial_value, 'mp', axis=1, tiled=True)  7.94 us
    gather x2, local copies, waits for them, and re-layouts, per_device(): jnp.take(vocab_basis, jnp.clip(local_ids, 0, vocab_rows - 1), axis=0)  7.42 us
    all_to_all x1, waiting for transfers between devices, per_device(): lax.all_to_all(targets, 'mp', split_axis=2, concat_axis=1, tiled=True)  5.79 us
    all_to_all x1, starting transfers between devices, per_device(): lax.all_to_all(targets, 'mp', split_axis=2, concat_axis=1, tiled=True)  3.71 us
  transfers between devices with their start and end apart: 2, of which 2 were waited for; matrix products, arithmetic and copies ran while one was open for 1% of the time, Pallas kernels for 0%

profile of v1, /device:TPU:0, one launch (start us, length us, event | category | flops | bytes accessed | tf_op | source)
XLA Modules:
  0.0 106.4 jit_solution(1835020389606034706)
XLA Ops:
  6.5 0.0 copy-start
  6.5 0.0 all-gather.4.cloned.1.call-start
  6.5 0.8 compare_and_fusion.1
  7.4 0.7 fusion.24
  8.1 7.3 %copy.31 = bf16[32064,32]{1,0:T(8,128)(2,1)} copy(bf16[32064,32]{0,1:T(8,128)(2,1)} %param.13) | data formatting | bytes 4104192 | tf_op args[3]
  15.4 0.0 copy-start.3
  15.4 0.0 copy-start.4
  15.4 7.3 %gather_fusion = bf16[1024,32]{1,0:T(8,128)(2,1)S(1)} fusion(bf16[32064,32]{1,0:T(8,128)(2,1)} %copy.31, s32[1024]{0:T(1024)S(1)} %fusion.24), kind=kCustom, calls=%fused_computation | custom fusion | bytes 135168 | tf_op jit(solution)/shard_map/jit(_take)/gather | solution.py:50
  22.7 0.1 copy.32
  22.8 0.0 copy-done
  22.8 0.0 copy-done.3
  22.8 0.0 copy-start.1
  22.8 0.0 copy-start.2
  22.8 0.0 copy-start.5
  22.8 0.7 fusion
  23.6 0.0 copy-done.4
  23.6 0.8 copy-done.1
  24.4 0.7 fusion.2
  25.1 0.0 copy-done.2
  25.1 0.0 copy-done.5
  25.1 0.0 copy-start.6
  25.1 0.0 copy-start.7
  25.2 0.7 fusion.25
  25.9 0.8 pad_maximum_fusion
  26.8 0.0 all-gather.4.cloned.1.call-update
  26.8 0.0 copy-done.6
  26.8 17.0 %all_gather.17 = bf16[2,256,256]{1,0,2:T(2,128)(2,1)} all-gather(bf16[2,256,32]{1,0,2:T(2,128)(2,1)S(1)} %copy.29), channel_id=1, replica_groups=mesh['dp'=8,'mp'=4] {'dp'}, dimensions={2}, use_global_device_ids=true | all-gather | bytes 294912 | tf_op jit(solution)/shard_map/all_gather | solution.py:68
  43.8 3.7 %all-to-all-start = ((bf16[2,256,256]{1,0,2:T(2,128)(2,1)}), bf16[2,256,256]{1,0,2:T(2,128)(2,1)S(1)}, u32[]{:S(2)}, u32[]{:S(2)}) async-start(bf16[2,256,256]{1,0,2:T(2,128)(2,1)} %all_gather.17), calls=%async_computation | async-start | bytes 524288 | tf_op jit(solution)/shard_map/all_to_all | solution.py:70
  47.5 0.0 copy-done.7
  47.5 0.1 fusion.23
  47.6 5.8 %all-to-all-done = bf16[2,256,256]{1,0,2:T(2,128)(2,1)S(1)} async-done(((bf16[2,256,256]{1,0,2:T(2,128)(2,1)}), bf16[2,256,256]{1,0,2:T(2,128)(2,1)S(1)}, u32[]{:S(2)}, u32[]{:S(2)}) %all-to-all-start) | async-done | bytes 262176 | tf_op jit(solution)/shard_map/all_to_all | solution.py:70
  53.4 0.2 copy.49
  53.6 0.2 all_to_all.16
  53.8 0.6 multiply_reduce_fusion.1
  54.4 10.6 %all-gather.4.cloned.1.call-done = f32[4096,128]{0,1:T(8,128)} async-done(((f32[1024,128]{0,1:T(8,128)}), f32[4096,128]{0,1:T(8,128)}) %all-gather.4.cloned.1.call-update) | async-done | bytes 2097168 | tf_op jit(solution)/shard_map/all_gather | solution.py:59
  64.9 3.6 %reshape.77 = f32[4,1024,128]{1,0,2:T(4,128)} reshape(f32[4096,128]{0,1:T(8,128)} %all-gather.4.cloned.1.call-done) | data formatting | bytes 4194304 | tf_op jit(solution)/shard_map/all_gather | solution.py:59
  68.6 2.9 %reduce_sum.45 = f32[1024,128]{0,1:T(8,128)S(1)} reduce(f32[4,1024,128]{1,0,2:T(4,128)} %reshape.77, f32[]{:T(128)} %constant.15.clone.1), dimensions={0}, to_apply=%region_0.1 | reduce | flops 393216 | bytes 2621444 | tf_op jit(solution)/shard_map/reduce_sum | solution.py:59
  71.4 0.1 copy.41
  71.6 0.6 fusion.14
  72.2 0.1 reshape.68
  72.3 14.8 %all_gather.18 = f32[2,64,1024]{2,1,0:T(8,128)S(1)} all-gather(f32[2,8,1024]{2,1,0:T(8,128)S(1)} %reshape.68), channel_id=1, replica_groups=mesh['dp'=8,'mp'=4] {'dp'}, dimensions={1}, use_global_device_ids=true | all-gather | bytes 589824 | tf_op jit(solution)/shard_map/all_gather | solution.py:69
  87.2 0.4 fusion.26
  87.6 0.8 fusion.8
  88.4 0.2 multiply_reduce_fusion
  88.6 0.7 fusion.19
  89.4 0.8 fusion.7
  90.2 0.7 convolution_bitcast_fusion
  90.9 7.9 %all-gather.1 = f32[4,64,8]{1,2,0:T(8,128)S(1)} all-gather(f32[1,64,8]{1,2,0:T(8,128)S(1)} %convolution_bitcast_fusion), channel_id=1, replica_groups=mesh['dp'=8,'mp'=4] {'mp'}, dimensions={0}, use_global_device_ids=true | all-gather | bytes 10240 | tf_op jit(solution)/shard_map/all_gather | solution.py:85
  98.8 0.7 reshape.80
  (9 shorter events, 0.1 us)
Async XLA Ops:
  6.5 16.2 %copy-start = (bf16[1,1024,1024]{2,1,0:T(8,128)(2,1)S(1)}, bf16[1,1024,1024]{2,1,0:T(8,128)(2,1)}, u32[]{:S(2)}) copy-start(bf16[1,1024,1024]{2,1,0:T(8,128)(2,1)} %param.15) | copy-start | bytes 6291460
  6.5 58.4 %all-gather.4.cloned.1.call-start = ((), (), s32[]{:S(2)}) async-start(), calls=%async_computation.1 | async-start | bytes 2621440 | tf_op jit(solution)/shard_map/all_gather | solution.py:59
  15.4 7.4 %copy-start.3 = (bf16[1,1024,32]{1,2,0:T(8,128)(2,1)S(1)}, bf16[1,1024,32]{1,2,0:T(8,128)(2,1)}, u32[]{:S(2)}) copy-start(bf16[1,1024,32]{1,2,0:T(8,128)(2,1)} %param.17) | copy-start | bytes 196612
  15.4 8.2 %copy-start.4 = (bf16[1,1024,32]{1,2,0:T(8,128)(2,1)S(1)}, bf16[1,1024,32]{1,2,0:T(8,128)(2,1)}, u32[]{:S(2)}) copy-start(bf16[1,1024,32]{1,2,0:T(8,128)(2,1)} %param.18) | copy-start | bytes 196612
  22.8 1.6 %copy-start.1 = (bf16[1,1024,1024]{2,1,0:T(8,128)(2,1)S(1)}, bf16[1,1024,1024]{2,1,0:T(8,128)(2,1)}, u32[]{:S(2)}) copy-start(bf16[1,1024,1024]{2,1,0:T(8,128)(2,1)} %param.16) | copy-start | bytes 6291460
  22.8 2.3 %copy-start.2 = (bf16[1024,1024]{1,0:T(8,128)(2,1)S(1)}, bf16[1024,1024]{1,0:T(8,128)(2,1)}, u32[]{:S(2)}) copy-start(bf16[1024,1024]{1,0:T(8,128)(2,1)} %param.12) | copy-start | bytes 6291460
  22.8 2.3 %copy-start.5 = (bf16[1024,32]{0,1:T(8,128)(2,1)S(1)}, bf16[1024,32]{0,1:T(8,128)(2,1)}, u32[]{:S(2)}) copy-start(bf16[1024,32]{0,1:T(8,128)(2,1)} %param.14) | copy-start | bytes 196612
  25.1 1.6 %copy-start.6 = (bf16[2,256,32]{1,2,0:T(8,128)(2,1)S(1)}, bf16[2,256,32]{1,2,0:T(8,128)(2,1)}, u32[]{:S(2)}) copy-start(bf16[2,256,32]{1,2,0:T(8,128)(2,1)} %param.19) | copy-start | bytes 98308
  25.1 22.4 %copy-start.7 = (s32[8]{0:T(128)S(1)}, s32[8]{0:T(128)}, u32[]{:S(2)}) copy-start(s32[8]{0:T(128)} %param.11) | copy-start | bytes 100
  43.8 9.6 %all-to-all-start = ((bf16[2,256,256]{1,0,2:T(2,128)(2,1)}), bf16[2,256,256]{1,0,2:T(2,128)(2,1)S(1)}, u32[]{:S(2)}, u32[]{:S(2)}) async-start(bf16[2,256,256]{1,0,2:T(2,128)(2,1)} %all_gather.17), calls=%async_computation | async-start | bytes 524288 | tf_op jit(solution)/shard_map/all_to_all | solution.py:70
Sparse Core Ops, SparseCore 0:
  26.9 38.0 all-gather.3
